TPU v7x, 32 devices: a whole 2x2x4 slice. The times are simulated.
32 devices in a mesh: band: 4 (over y, core), grid: 8 (over z, x).
Axes of the slice: x: 2, y: 2, z: 4, core: 2. Of those that a mesh axis runs over, the one named last changes fastest.
Arguments:
- orbitals: bfloat16 [64, 2, 16, 128, 128], P('band', None, 'grid'), may hold values from -1.5 to 1.5
- occupations: float32 [64], P('band'), may hold values from 0.2 to 2
Outputs:
- current: float32 [3, 16, 128, 128], P(None, 'grid', 'band')
All inputs are finite; a program needn't handle non-finite values.
Results may differ from a plain program's by a relative error of at most 0.0003.
Values may be sent and summed in bfloat16 or wider, within the bound.
A program may use at most 64 MiB of HBM per device.

v0:
```python
import math

import jax
import jax.numpy as jnp
from jax import lax
from jax.sharding import PartitionSpec as P


def extended(cells, sides, width):
    for axis, dim in sides:
        count = lax.axis_size(axis)
        head = lax.slice_in_dim(cells, 0, width, axis=dim)
        tail = lax.slice_in_dim(cells, cells.shape[dim] - width, cells.shape[dim], axis=dim)
        cells = jnp.concatenate(
            [
                lax.ppermute(tail, axis, [(i, (i + 1) % count) for i in range(count)]),
                cells,
                lax.ppermute(head, axis, [((i + 1) % count, i) for i in range(count)]),
            ],
            axis=dim,
        )
    return cells


def derivative(values, direction):
    forward = jnp.roll(values, -1, direction) - jnp.roll(values, 1, direction)
    farther = jnp.roll(values, -2, direction) - jnp.roll(values, 2, direction)
    return (8.0 * forward - farther) / 12.0


def vertical(widened, depth_cells):
    forward = widened[:, 3 : 3 + depth_cells] - widened[:, 1 : 1 + depth_cells]
    farther = widened[:, 4 : 4 + depth_cells] - widened[:, 0:depth_cells]
    return (8.0 * forward - farther) / 12.0


def band_sum(orbitals, weights, padded, with_depth, lateral):
    bands = orbitals.shape[0]
    depth_cells = orbitals.shape[2]
    block_size = math.gcd(bands, 8)
    parts_count = (1 if with_depth else 0) + (2 if lateral else 0)

    def advance(block_index, summed):
        offset = block_index * block_size
        center = lax.dynamic_slice_in_dim(orbitals, offset, block_size, 0).astype(jnp.float32)
        factors = lax.dynamic_slice_in_dim(weights, offset, block_size, 0)
        real_part = center[:, 0]
        imag_part = center[:, 1]
        terms = []
        if with_depth:
            widened = lax.dynamic_slice_in_dim(padded, offset, block_size, 0).astype(jnp.float32)
            terms.append(
                real_part * vertical(widened[:, 1], depth_cells)
                - imag_part * vertical(widened[:, 0], depth_cells)
            )
        if lateral:
            for direction in (2, 3):
                terms.append(
                    real_part * derivative(imag_part, direction)
                    - imag_part * derivative(real_part, direction)
                )
        stacked = jnp.stack(terms)
        return summed + jnp.sum(factors[None, :, None, None, None] * stacked, 1)

    initial = jnp.zeros(
        (parts_count, depth_cells, orbitals.shape[3], orbitals.shape[4]), jnp.float32
    )
    return lax.fori_loop(0, bands // block_size, advance, initial)


def depth_part(orbitals, weights):
    padded = extended(orbitals, (("grid", 2),), 2)
    return band_sum(orbitals, weights, padded, True, False)


def per_device(orbitals, occupations):
    lateral_part = band_sum(orbitals, occupations, None, False, True)
    plane_sums = lax.psum_scatter(lateral_part, "band", scatter_dimension=2, tiled=True)
    depth_sums = lax.psum_scatter(
        depth_part(orbitals, occupations), "band", scatter_dimension=2, tiled=True
    )
    return jnp.concatenate([depth_sums, plane_sums], 0)


def solution(mesh):
    placed = (P("band", None, "grid", None, None), P("band"))
    return jax.shard_map(
        per_device,
        mesh=mesh,
        in_specs=placed,
        out_specs=P(None, "grid", "band", None),
        check_vma=False,
    )
```

profile of v0, /device:TPU:0, one launch (start us, length us, event | category | flops | bytes accessed | tf_op | source)
XLA Modules:
  0.0 149.4 jit_solution(17086221204871014268)
XLA Ops:
  6.5 3.3 %copy.34 = bf16[16,2,2,128,128]{4,3,2,0,1:T(8,128)(2,1)} copy(bf16[16,2,2,128,128]{4,3,2,1,0:T(8,128)(2,1)} %param.6) | data formatting | bytes 4194304 | tf_op args[0]
  9.9 6.0 %collective-permute-start.1 = (bf16[16,2,2,128,128]{4,3,2,0,1:T(8,128)(2,1)}, bf16[16,2,2,128,128]{4,3,2,0,1:T(8,128)(2,1)}, u32[]{:S(2)}, u32[]{:S(2)}) collective-permute-start(bf16[16,2,2,128,128]{4,3,2,0,1:T(8,128)(2,1)} %copy.34), channel_id=1, source_target_pairs={{1,0},{2,1},{3,2},{4,3},{5,4},{6,5},{7,6},{0,7},{9,8},{10,9},{11,1... | collective-permute-start | bytes 6291464 | tf_op jit(solution)/shard_map/ppermute | solution.py:18
  15.9 66.2 %while.29 = (s32[]{:T(128)}, f32[2,2,128,128]{3,2,1,0:T(8,128)S(1)}, f32[16]{0:T(128)S(1)}, bf16[16,2,2,128,128]{4,3,2,1,0:T(8,128)(2,1)S(1)}, s32[]{:T(128)}, /...) while((s32[]{:T(128)}, f32[2,2,128,128]{3,2,1,0:T(8,128)S(1)}, ...), condition=%wide.region_6.7_spmd.clone, body=%wide.region_4.6_spmd.clone.sunk | while | flops 13172743 | bytes 94503256 | solution.py:68
  18.0 2.3 %fusion.42 = (f32[8,2,128,1]{3,0,2,1:T(8,128)}, f32[8,2,128,1]{3,0,2,1:T(8,128)}, f32[8,2,128,1]{3,0,2,1:T(8,128)S(1)}, f32[8,2,128,1]{3,0,2,1:T(8,128)}) fusion(f32[8,2,128,128]{3,0,2,1:T(8,128)S(1)} %get-tuple-element.385, f32[8,2,128,128]{3,0,2,1:T(8,128)S(1)} %get-tuple-element.386), kind=kLoop, calls=%fused_computation.85.clone.1 | loop fusion | bytes 65536 | tf_op jit(solution)/shard_map/while/body/eval_jaxpr/jit(_roll_static)/slice | solution.py:26
  21.0 2.5 %slice_bitcast_fusion.45 = (f32[1,8,2,128,127]{4,1,3,2,0:T(8,128)}, f32[1,8,2,128,127]{4,1,3,2,0:T(8,128)}, f32[1,8,2,128,127]{4,1,3,2,0:T(8,128)}, f32[1,8,2,128,127]{4,1,3,2,0:T(8,128)}) fusion(f32[8,2,128,128]{3,0,2,1:T(8,128)S(1)} %get-tuple-element.385, f32[8,2,128,128]{3,0,2,1:T(8,128)S(1)} %get-tuple-element.386), kind=kLoop, calls=%fused_computation.28.clone.1 | loop fusion | bytes 8323072 | tf_op jit(solution)/shard_map/while/body/eval_jaxpr/jit(_roll_static)/concatenate | solution.py:26
  23.6 1.6 %copy.58 = f32[8,2,128,1]{2,0,3,1:T(8,128)S(1)} copy(f32[8,2,128,1]{3,0,2,1:T(8,128)} %get-tuple-element.390) | data formatting | bytes 16384 | tf_op jit(solution)/shard_map/while/body/eval_jaxpr/jit(_roll_static)/slice | solution.py:26
  26.5 2.6 %slice_bitcast_fusion.46 = (f32[1,8,2,128,2]{4,1,3,2,0:T(8,128)}, f32[1,8,2,128,2]{4,1,3,2,0:T(8,128)}, f32[1,8,2,128,2]{4,1,3,2,0:T(8,128)}, f32[1,8,2,128,2]{4,1,3,2,0:T(8,128)}) fusion(f32[8,2,128,128]{3,0,2,1:T(8,128)S(1)} %get-tuple-element.385, f32[8,2,128,128]{3,0,2,1:T(8,128)S(1)} %get-tuple-element.386), kind=kLoop, calls=%fused_computation.25.clone.1 | loop fusion | bytes 131072 | tf_op jit(solution)/shard_map/while/body/eval_jaxpr/jit(_roll_static)/concatenate | solution.py:27
  29.0 2.6 %slice_bitcast_fusion.47 = (f32[1,8,2,128,126]{4,1,3,2,0:T(8,128)}, f32[1,8,2,128,126]{4,1,3,2,0:T(8,128)}, f32[1,8,2,128,126]{4,1,3,2,0:T(8,128)}, f32[1,8,2,128,126]{4,1,3,2,0:T(8,128)}) fusion(f32[8,2,128,128]{3,0,2,1:T(8,128)S(1)} %get-tuple-element.385, f32[8,2,128,128]{3,0,2,1:T(8,128)S(1)} %get-tuple-element.386), kind=kLoop, calls=%fused_computation.24.clone.1 | loop fusion | bytes 8257536 | tf_op jit(solution)/shard_map/while/body/eval_jaxpr/jit(_roll_static)/concatenate | solution.py:27
  31.7 1.6 %copy.60 = f32[8,2,128,1]{2,0,3,1:T(8,128)S(1)} copy(f32[8,2,128,1]{3,0,2,1:T(8,128)} %get-tuple-element.395) | data formatting | bytes 16384 | tf_op jit(solution)/shard_map/while/body/eval_jaxpr/jit(_roll_static)/slice | solution.py:26
  34.6 1.6 %copy.62 = f32[8,2,128,1]{2,0,3,1:T(8,128)S(1)} copy(f32[8,2,128,1]{3,0,2,1:T(8,128)} %get-tuple-element.398) | data formatting | bytes 16384 | tf_op jit(solution)/shard_map/while/body/eval_jaxpr/jit(_roll_static)/slice | solution.py:26
  37.6 7.3 %fusion.43 = f32[1,8,2,128,128]{4,1,3,2,0:T(8,128)S(1)} fusion(f32[1,8,2,128,1]{4,1,3,2,0:T(8,128)S(1)} %copy.57, f32[1,8,2,128,127]{4,1,3,2,0:T(8,128)} %get-tuple-element.388, f32[1,8,2,128,127]{4,1,3,2,0:T(8,128)} %get-tuple-element.389, f32[1,8,2,128,1]{4,1,3,2,0:T(8,128)} %copy.59, f32[1,8,2,128,2]{4,1,3,2,0:T(8,128)} %get-tuple-element.391, ...), kind=kLoop, calls=%fused_computation.54.clone.1 | loop fusion | flops 5505024 | bytes 11534336 | tf_op jit(solution)/shard_map/while/body/eval_jaxpr/sub | solution.py:59
  51.0 2.3 %fusion.42 = (f32[8,2,128,1]{3,0,2,1:T(8,128)}, f32[8,2,128,1]{3,0,2,1:T(8,128)}, f32[8,2,128,1]{3,0,2,1:T(8,128)S(1)}, f32[8,2,128,1]{3,0,2,1:T(8,128)}) fusion(f32[8,2,128,128]{3,0,2,1:T(8,128)S(1)} %get-tuple-element.385, f32[8,2,128,128]{3,0,2,1:T(8,128)S(1)} %get-tuple-element.386), kind=kLoop, calls=%fused_computation.85.clone.1 | loop fusion | bytes 65536 | tf_op jit(solution)/shard_map/while/body/eval_jaxpr/jit(_roll_static)/slice | solution.py:26
  54.1 2.5 %slice_bitcast_fusion.45 = (f32[1,8,2,128,127]{4,1,3,2,0:T(8,128)}, f32[1,8,2,128,127]{4,1,3,2,0:T(8,128)}, f32[1,8,2,128,127]{4,1,3,2,0:T(8,128)}, f32[1,8,2,128,127]{4,1,3,2,0:T(8,128)}) fusion(f32[8,2,128,128]{3,0,2,1:T(8,128)S(1)} %get-tuple-element.385, f32[8,2,128,128]{3,0,2,1:T(8,128)S(1)} %get-tuple-element.386), kind=kLoop, calls=%fused_computation.28.clone.1 | loop fusion | bytes 8323072 | tf_op jit(solution)/shard_map/while/body/eval_jaxpr/jit(_roll_static)/concatenate | solution.py:26
  56.7 1.6 %copy.58 = f32[8,2,128,1]{2,0,3,1:T(8,128)S(1)} copy(f32[8,2,128,1]{3,0,2,1:T(8,128)} %get-tuple-element.390) | data formatting | bytes 16384 | tf_op jit(solution)/shard_map/while/body/eval_jaxpr/jit(_roll_static)/slice | solution.py:26
  59.6 2.6 %slice_bitcast_fusion.46 = (f32[1,8,2,128,2]{4,1,3,2,0:T(8,128)}, f32[1,8,2,128,2]{4,1,3,2,0:T(8,128)}, f32[1,8,2,128,2]{4,1,3,2,0:T(8,128)}, f32[1,8,2,128,2]{4,1,3,2,0:T(8,128)}) fusion(f32[8,2,128,128]{3,0,2,1:T(8,128)S(1)} %get-tuple-element.385, f32[8,2,128,128]{3,0,2,1:T(8,128)S(1)} %get-tuple-element.386), kind=kLoop, calls=%fused_computation.25.clone.1 | loop fusion | bytes 131072 | tf_op jit(solution)/shard_map/while/body/eval_jaxpr/jit(_roll_static)/concatenate | solution.py:27
  62.1 2.6 %slice_bitcast_fusion.47 = (f32[1,8,2,128,126]{4,1,3,2,0:T(8,128)}, f32[1,8,2,128,126]{4,1,3,2,0:T(8,128)}, f32[1,8,2,128,126]{4,1,3,2,0:T(8,128)}, f32[1,8,2,128,126]{4,1,3,2,0:T(8,128)}) fusion(f32[8,2,128,128]{3,0,2,1:T(8,128)S(1)} %get-tuple-element.385, f32[8,2,128,128]{3,0,2,1:T(8,128)S(1)} %get-tuple-element.386), kind=kLoop, calls=%fused_computation.24.clone.1 | loop fusion | bytes 8257536 | tf_op jit(solution)/shard_map/while/body/eval_jaxpr/jit(_roll_static)/concatenate | solution.py:27
  64.8 1.6 %copy.60 = f32[8,2,128,1]{2,0,3,1:T(8,128)S(1)} copy(f32[8,2,128,1]{3,0,2,1:T(8,128)} %get-tuple-element.395) | data formatting | bytes 16384 | tf_op jit(solution)/shard_map/while/body/eval_jaxpr/jit(_roll_static)/slice | solution.py:26
  70.7 7.3 %fusion.43 = f32[1,8,2,128,128]{4,1,3,2,0:T(8,128)S(1)} fusion(f32[1,8,2,128,1]{4,1,3,2,0:T(8,128)S(1)} %copy.57, f32[1,8,2,128,127]{4,1,3,2,0:T(8,128)} %get-tuple-element.388, f32[1,8,2,128,127]{4,1,3,2,0:T(8,128)} %get-tuple-element.389, f32[1,8,2,128,1]{4,1,3,2,0:T(8,128)} %copy.59, f32[1,8,2,128,2]{4,1,3,2,0:T(8,128)} %get-tuple-element.391, ...), kind=kLoop, calls=%fused_computation.54.clone.1 | loop fusion | flops 5505024 | bytes 11534336 | tf_op jit(solution)/shard_map/while/body/eval_jaxpr/sub | solution.py:59
  82.9 20.8 %collective-permute-done.1 = bf16[16,2,2,128,128]{4,3,2,0,1:T(8,128)(2,1)} collective-permute-done((bf16[16,2,2,128,128]{4,3,2,0,1:T(8,128)(2,1)}, bf16[16,2,2,128,128]{4,3,2,0,1:T(8,128)(2,1)}, u32[]{:S(2)}, u32[]{:S(2)}) %collective-permute-start.1) | collective-permute-done | bytes 2097184 | tf_op jit(solution)/shard_map/ppermute | solution.py:18
  103.9 5.4 %pad_maximum_fusion = bf16[16,2,6,128,128]{4,3,2,0,1:T(8,128)(2,1)} fusion(bf16[16,2,2,128,128]{4,3,2,0,1:T(8,128)(2,1)} %collective-permute-done.1, bf16[16,2,2,128,128]{4,3,2,0,1:T(8,128)(2,1)} %collective-permute-done, bf16[16,2,2,128,128]{4,3,2,1,0:T(8,128)(2,1)S(1)} %get-tuple-element.475), kind=kLoop, calls=%fused_computation.83 | loop fusion | flops 18874368 | bytes 12582912 | tf_op jit(solution)/shard_map/concatenate | solution.py:14
  109.3 9.7 %while.28 = (s32[]{:T(128)}, f32[1,2,128,128]{3,2,1,0:T(8,128)S(1)}, f32[16]{0:T(128)S(1)}, bf16[16,2,2,128,128]{4,3,2,1,0:T(8,128)(2,1)S(1)}, bf16[16,2,6,128,1...) while((s32[]{:T(128)}, f32[1,2,128,128]{3,2,1,0:T(8,128)S(1)}, ...), condition=%wide.region_2.3_spmd.clone, body=%wide.region_0.2_spmd.clone.sunk | while | flops 6062087 | bytes 36176136 | solution.py:68
  109.3 2.7 %dynamic-slice_convert_fusion.4 = f32[8,2,6,128,128]{4,3,2,0,1:T(8,128)S(1)} fusion(bf16[16,2,6,128,128]{4,3,2,0,1:T(8,128)(2,1)} %get-tuple-element.465, s32[]{:T(128)S(6)} %select_n.21), kind=kLoop, calls=%fused_computation.2.clone.1 | loop fusion | flops 1572864 | bytes 9437188 | tf_op jit(solution)/shard_map/while/body/eval_jaxpr/convert_element_type | solution.py:51
  114.2 2.7 %dynamic-slice_convert_fusion.4 = f32[8,2,6,128,128]{4,3,2,0,1:T(8,128)S(1)} fusion(bf16[16,2,6,128,128]{4,3,2,0,1:T(8,128)(2,1)} %get-tuple-element.465, s32[]{:T(128)S(6)} %select_n.21), kind=kLoop, calls=%fused_computation.2.clone.1 | loop fusion | flops 1572864 | bytes 9437188 | tf_op jit(solution)/shard_map/while/body/eval_jaxpr/convert_element_type | solution.py:51
  119.7 21.4 %reduce-scatter.3.cloned.1.call-done = f32[1,2,32,128]{3,2,1,0:T(8,128)} async-done(((f32[1,2,128,128]{3,2,1,0:T(8,128)}), f32[1,2,32,128]{3,2,1,0:T(8,128)}) %reduce-scatter.3.cloned.1.call-update) | async-done | bytes 32784 | tf_op jit(solution)/shard_map/reduce_scatter | solution.py:79
  (73 shorter events, 30.9 us)
Async XLA Ops:
  6.5 9.3 %copy-start.2 = (bf16[16,2,2,128,128]{4,3,2,1,0:T(8,128)(2,1)S(1)}, bf16[16,2,2,128,128]{4,3,2,1,0:T(8,128)(2,1)}, u32[]{:S(2)}) copy-start(bf16[16,2,2,128,128]{4,3,2,1,0:T(8,128)(2,1)} %param.6) | copy-start | bytes 6291460
  6.5 9.3 %copy-start.6 = (f32[16]{0:T(128)S(1)}, f32[16]{0:T(128)}, u32[]{:S(2)}) copy-start(f32[16]{0:T(128)} %param.7) | copy-start | bytes 196
  6.5 113.2 %reduce-scatter.5.cloned.1.call-start = ((), (), s32[]{:S(2)}) async-start(), calls=%async_computation.3 | async-start | bytes 327680 | tf_op jit(solution)/shard_map/reduce_scatter | solution.py:78
  9.9 93.9 %collective-permute-start.1 = (bf16[16,2,2,128,128]{4,3,2,0,1:T(8,128)(2,1)}, bf16[16,2,2,128,128]{4,3,2,0,1:T(8,128)(2,1)}, u32[]{:S(2)}, u32[]{:S(2)}) collective-permute-start(bf16[16,2,2,128,128]{4,3,2,0,1:T(8,128)(2,1)} %copy.34), channel_id=1, source_target_pairs={{1,0},{2,1},{3,2},{4,3},{5,4},{6,5},{7,6},{0,7},{9,8},{10,9},{11,1... | collective-permute-start | bytes 6291464 | tf_op jit(solution)/shard_map/ppermute | solution.py:18
  15.9 88.0 %collective-permute-start = (bf16[16,2,2,128,128]{4,3,2,0,1:T(8,128)(2,1)}, bf16[16,2,2,128,128]{4,3,2,0,1:T(8,128)(2,1)}, u32[]{:S(2)}, u32[]{:S(2)}) collective-permute-start(bf16[16,2,2,128,128]{4,3,2,0,1:T(8,128)(2,1)} %copy.34), channel_id=1, source_target_pairs={{0,1},{1,2},{2,3},{3,4},{4,5},{5,6},{6,7},{7,0},{8,9},{9,10},{10,1... | collective-permute-start | bytes 6291464 | tf_op jit(solution)/shard_map/ppermute | solution.py:16
  16.6 1.3 copy-start
  45.2 1.6 %copy-start.1 = (f32[8,2,2,128,128]{4,0,3,2,1:T(8,128)S(1)}, f32[8,2,2,128,128]{4,0,3,2,1:T(8,128)}, u32[]{:S(2)}) copy-start(f32[8,2,2,128,128]{4,0,3,2,1:T(8,128)} %copy-done) | copy-start | bytes 6291460 | tf_op jit(solution)/shard_map/while
  47.4 1.6 %copy-start.3 = (bf16[16,2,2,128,128]{4,3,2,1,0:T(8,128)(2,1)S(1)}, bf16[16,2,2,128,128]{4,3,2,1,0:T(8,128)(2,1)}, u32[]{:S(2)}) copy-start(bf16[16,2,2,128,128]{4,3,2,1,0:T(8,128)(2,1)} %get-tuple-element.480) | copy-start | bytes 6291460 | tf_op jit(solution)/shard_map/while
  49.7 1.3 copy-start
  78.3 1.6 %copy-start.1 = (f32[8,2,2,128,128]{4,0,3,2,1:T(8,128)S(1)}, f32[8,2,2,128,128]{4,0,3,2,1:T(8,128)}, u32[]{:S(2)}) copy-start(f32[8,2,2,128,128]{4,0,3,2,1:T(8,128)} %copy-done) | copy-start | bytes 6291460 | tf_op jit(solution)/shard_map/while
  80.5 1.6 %copy-start.3 = (bf16[16,2,2,128,128]{4,3,2,1,0:T(8,128)(2,1)S(1)}, bf16[16,2,2,128,128]{4,3,2,1,0:T(8,128)(2,1)}, u32[]{:S(2)}) copy-start(bf16[16,2,2,128,128]{4,3,2,1,0:T(8,128)(2,1)} %get-tuple-element.480) | copy-start | bytes 6291460 | tf_op jit(solution)/shard_map/while
  82.1 0.7 copy-start.4
  82.8 58.3 %reduce-scatter.3.cloned.1.call-start = ((), (), s32[]{:S(2)}) async-start(), calls=%async_computation.2 | async-start | bytes 163840 | tf_op jit(solution)/shard_map/reduce_scatter | solution.py:79
  119.0 0.7 copy-start.5
Sparse Core Ops, SparseCore 0:
  83.0 21.4 reduce-scatter.4
  119.8 21.2 reduce-scatter.2
where the time goes:
time: 150 us; the launch traced here: 149 us
  local copies, waits for them, and re-layouts  53.9 us (36%)
  waiting for transfers between devices  42.4 us (28%)
  other arithmetic  33.3 us (22%)
  between operations  13.4 us (9%)
  starting transfers between devices  6.05 us (4%)
    reduce_scatter x1, waiting for transfers between devices, per_device(): lax.psum_scatter(depth_part(orbitals, occupations), 'band', scatter_dimen...  21.4 us
    ppermute x1, waiting for transfers between devices, extended(): lax.ppermute(head, axis, [((i + 1) % count, i) for i in range(count)])  20.8 us
    sub x4, other arithmetic, advance(): real_part * derivative(imag_part, direction)  15.8 us
    concatenate x14, local copies, waits for them, and re-layouts, derivative(): forward = jnp.roll(values, -1, direction) - jnp.roll(values, 1, direction)  14.9 us
    slice x10, local copies, waits for them, and re-layouts, derivative(): forward = jnp.roll(values, -1, direction) - jnp.roll(values, 1, direction)  14.6 us
    concatenate x8, local copies, waits for them, and re-layouts, derivative(): farther = jnp.roll(values, -2, direction) - jnp.roll(values, 2, direction)  10.9 us
    while x12, local copies, waits for them, and re-layouts  6.42 us
    ppermute x1, starting transfers between devices, extended(): lax.ppermute(head, axis, [((i + 1) % count, i) for i in range(count)])  6 us
  transfers between devices with their start and end apart: 4, of which 3 were waited for; matrix products, arithmetic and copies ran while one was open for 50% of the time, Pallas kernels for 0%

commit v1 on v0

v1 whole, which is shorter than its diff:
```python
import functools

import jax
import jax.numpy as jnp
from jax import lax
from jax.experimental import pallas as pl
from jax.experimental.pallas import tpu as pltpu
from jax.sharding import PartitionSpec as P

CHUNK = 16


def stencil(n, flipped):
    row = lax.broadcasted_iota(jnp.int32, (n, n), 0)
    col = lax.broadcasted_iota(jnp.int32, (n, n), 1)
    d = col - row if flipped else row - col
    value = jnp.zeros((n, n), jnp.float32)
    for step, weight in ((1, 8.0), (-1, -8.0), (2, -1.0), (-2, 1.0)):
        hit = (d == step) | (d == step - n) | (d == step + n)
        value = jnp.where(hit, weight, value)
    return value.astype(jnp.bfloat16)


def kernel(
    nb, ng, occ_ref, orb_ref, out_ref,
    own, mate, outer, mx, my, plane_sum, plane_recv, zsend, zrecv,
    own_sem, mate_send, mate_recv, outer_send, outer_recv,
    plane_send_sem, plane_recv_sem, z_send_sem, z_recv_sem,
):
    bands, _, depth, nx, ny = orb_ref.shape
    b = lax.axis_index("band")
    g = lax.axis_index("grid")
    odd = lax.rem(g, 2)
    turn = 1 - 2 * odd
    partner = g + turn
    ahead = lax.rem(g + 2 * turn + ng, ng)
    behind = lax.rem(g - 2 * turn + ng, ng)
    rows = nx // nb
    subs = rows // CHUNK
    chunks = (nb // 2) * subs

    load = pltpu.make_async_copy(orb_ref, own, own_sem)
    load.start()

    barrier = pltpu.get_barrier_semaphore()
    count = 0
    for k in range(nb):
        peer = lax.rem(b + k, nb)
        for at in (g, partner, ahead, behind):
            if k == 0 and at is g:
                continue
            pl.semaphore_signal(barrier, inc=1, device_id={"band": peer, "grid": at})
            count += 1
    pl.semaphore_wait(barrier, count)

    def start_of(chunk, parity):
        block = (chunk // subs) * 2 + parity
        return pl.multiple_of(block * rows + (chunk % subs) * CHUNK, CHUNK)

    def to_mate(c):
        return pltpu.make_async_remote_copy(
            src_ref=orb_ref.at[:, :, :, pl.ds(start_of(c, 1 - odd), CHUNK), :],
            dst_ref=mate.at[c],
            send_sem=mate_send.at[c],
            recv_sem=mate_recv.at[c],
            device_id={"band": b, "grid": partner},
        )

    def to_outer(c):
        return pltpu.make_async_remote_copy(
            src_ref=orb_ref.at[:, :, :, pl.ds(start_of(c, odd), CHUNK), :],
            dst_ref=outer.at[c],
            send_sem=outer_send.at[c],
            recv_sem=outer_recv.at[c],
            device_id={"band": b, "grid": behind},
        )

    for c in range(chunks):
        to_mate(c).start()
        to_outer(c).start()

    mx[...] = stencil(nx, True)
    my[...] = stencil(ny, False)
    plane_sum[...] = jnp.zeros_like(plane_sum)
    load.wait()

    def lateral(n, carry):
        w = occ_ref[n]
        for s in range(depth):
            re = own[n, 0, s]
            im = own[n, 1, s]
            tx = jnp.dot(mx[...], jnp.concatenate([re, im], 1), preferred_element_type=jnp.float32)
            ty = jnp.dot(jnp.concatenate([re, im], 0), my[...], preferred_element_type=jnp.float32)
            wre = re.astype(jnp.float32) * w
            wim = im.astype(jnp.float32) * w
            plane_sum[0, s] += wre * tx[:, ny:] - wim * tx[:, :ny]
            plane_sum[1, s] += wre * ty[nx:] - wim * ty[:nx]
        return carry

    lax.fori_loop(0, bands, lateral, 0)

    def to_peer(k):
        peer = lax.rem(b + k, nb)
        return pltpu.make_async_remote_copy(
            src_ref=plane_sum.at[:, :, pl.ds(pl.multiple_of(peer * rows, rows), rows), :],
            dst_ref=plane_recv.at[k - 1],
            send_sem=plane_send_sem.at[k - 1],
            recv_sem=plane_recv_sem.at[k - 1],
            device_id={"band": peer, "grid": g},
        )

    for k in range(1, nb):
        to_peer(k).start()

    sign = turn.astype(jnp.float32)
    first = odd
    second = 1 - odd

    def to_owner(c, slab):
        at = (g, partner, ahead)[slab]
        sub = c % subs
        return pltpu.make_async_remote_copy(
            src_ref=zsend.at[c, slab],
            dst_ref=zrecv.at[slab // 2, b, :, pl.ds(sub * CHUNK, CHUNK), :],
            send_sem=z_send_sem.at[c, slab],
            recv_sem=z_recv_sem.at[slab // 2, b, sub],
            device_id={"band": (c // subs) * 2 + odd, "grid": at},
        )

    for c in range(chunks):
        start = start_of(c, odd)
        to_mate(c).wait_recv()
        to_outer(c).wait_recv()

        def depthwise(n, sums):
            w = occ_ref[n] * sign
            fields = []
            for p in (first, second):
                fields.append(tuple(own[n, q, p, pl.ds(start, CHUNK), :].astype(jnp.float32) for q in (0, 1)))
            for held in (mate, outer):
                for p in (first, second):
                    fields.append(tuple(held[c, n, q, p].astype(jnp.float32) for q in (0, 1)))
            scaled = [(re * w, im * w) for re, im in fields[:4]]
            pairs = ((0, 1), (1, 2), (2, 3), (3, 4), (0, 2), (1, 3), (2, 4), (3, 5))
            return tuple(
                total + (scaled[i][0] * fields[j][1] - scaled[i][1] * fields[j][0])
                for total, (i, j) in zip(sums, pairs)
            )

        zero = jnp.zeros((CHUNK, ny), jnp.float32)
        n01, n12, n23, n34, f02, f13, f24, f35 = lax.fori_loop(0, bands, depthwise, (zero,) * 8)
        parts = (
            (8.0 * n01 - f02, 8.0 * (n01 + n12) - f13),
            (8.0 * (n12 + n23) - f02 - f24, 8.0 * (n23 + n34) - f13 - f35),
            (8.0 * n34 - f24, -f35),
        )
        owner = (c // subs) * 2 + odd
        for slab in (1, 2, 0):
            zsend[c, slab, first] = parts[slab][0]
            zsend[c, slab, second] = parts[slab][1]
            if slab:
                to_owner(c, slab).start()
            else:
                @pl.when(owner != b)
                def _():
                    to_owner(c, 0).start()

                @pl.when(owner == b)
                def _():
                    here = pl.ds((c % subs) * CHUNK, CHUNK)
                    zrecv[0, b, first, here, :] = parts[0][0]
                    zrecv[0, b, second, here, :] = parts[0][1]

    mine = pl.ds(pl.multiple_of(b * rows, rows), rows)
    summed = plane_sum[:, :, mine, :]
    for k in range(1, nb):
        to_peer(k).wait_recv()
        summed = summed + plane_recv[k - 1]
    out_ref[1:3] = summed * (1.0 / 12.0)

    def arrival(kind, source):
        for sub in range(subs):
            pltpu.make_async_remote_copy(
                src_ref=zsend.at[0, 0],
                dst_ref=zrecv.at[kind, source, :, pl.ds(sub * CHUNK, CHUNK), :],
                send_sem=z_send_sem.at[0, 0],
                recv_sem=z_recv_sem.at[kind, source, sub],
                device_id={"band": b, "grid": partner},
            ).wait_recv()

    alike = lax.rem(b, 2) == odd

    @pl.when(alike)
    def _():
        for source in range(nb):
            @pl.when(b != source)
            def _():
                arrival(0, source)
        for source in range(nb):
            arrival(1, source)
        out_ref[0] = (jnp.sum(zrecv[0], 0) + jnp.sum(zrecv[1], 0)) * (1.0 / 12.0)

    @pl.when(jnp.logical_not(alike))
    def _():
        for source in range(nb):
            arrival(0, source)
        out_ref[0] = jnp.sum(zrecv[0], 0) * (1.0 / 12.0)

    for k in range(1, nb):
        to_peer(k).wait_send()
    for c in range(chunks):
        to_mate(c).wait_send()
        to_outer(c).wait_send()
        to_owner(c, 1).wait_send()
        to_owner(c, 2).wait_send()

        @pl.when((c // subs) * 2 + odd != b)
        def _():
            to_owner(c, 0).wait_send()


def solution(mesh):
    nb = mesh.shape["band"]
    ng = mesh.shape["grid"]

    def per_device(orbitals, occupations):
        bands, _, depth, nx, ny = orbitals.shape
        rows = nx // nb
        if depth != 2 or nb % 2 or ng % 2 or ng < 4 or rows % CHUNK:
            raise ValueError("unsupported sizes")
        subs = rows // CHUNK
        chunks = (nb // 2) * subs
        f32, bf16 = jnp.float32, jnp.bfloat16
        dma = pltpu.SemaphoreType.DMA
        return pl.pallas_call(
            functools.partial(kernel, nb, ng),
            out_shape=jax.ShapeDtypeStruct((3, depth, rows, ny), f32),
            in_specs=[
                pl.BlockSpec(memory_space=pltpu.SMEM),
                pl.BlockSpec(memory_space=pl.ANY),
            ],
            out_specs=pl.BlockSpec(memory_space=pltpu.VMEM),
            scratch_shapes=[
                pltpu.VMEM((bands, 2, depth, nx, ny), bf16),
                pltpu.VMEM((chunks, bands, 2, depth, CHUNK, ny), bf16),
                pltpu.VMEM((chunks, bands, 2, depth, CHUNK, ny), bf16),
                pltpu.VMEM((nx, nx), bf16),
                pltpu.VMEM((ny, ny), bf16),
                pltpu.VMEM((2, depth, nx, ny), f32),
                pltpu.VMEM((nb - 1, 2, depth, rows, ny), f32),
                pltpu.VMEM((chunks, 3, depth, CHUNK, ny), f32),
                pltpu.VMEM((2, nb, depth, rows, ny), f32),
                dma,
                dma((chunks,)),
                dma((chunks,)),
                dma((chunks,)),
                dma((chunks,)),
                dma((nb - 1,)),
                dma((nb - 1,)),
                dma((chunks, 3)),
                dma((2, nb, subs)),
            ],
            compiler_params=pltpu.CompilerParams(collective_id=0, has_side_effects=True),
            name="current",
        )(occupations, orbitals)

    return jax.shard_map(
        per_device,
        mesh=mesh,
        in_specs=(P("band", None, "grid", None, None), P("band")),
        out_specs=P(None, "grid", "band", None),
        check_vma=False,
    )
```

time: 150 us -> 38.3 us (0.26)
  the two profiles are of different devices: /device:TPU:0 before, /device:TPU:4 now
where the time goes in v1:
time: 38.3 us; the launch traced here: 38.1 us
  Pallas kernels  36.6 us (96%)
  local copies, waits for them, and re-layouts  1.54 us (4%)
    pallas_call x1, Pallas kernels, per_device(): pl.pallas_call(functools.partial(kernel, nb, ng), out_shape=jax.ShapeDtyp...  36.6 us
    unnamed x1, local copies, waits for them, and re-layouts  1.54 us

profile of v1, /device:TPU:4, one launch (start us, length us, event | category | flops | bytes accessed | tf_op | source)
XLA Modules:
  0.0 38.1 jit_solution(15150977709321343057)
XLA Ops:
  0.0 36.6 %current.1 = f32[3,2,32,128]{3,2,1,0:T(8,128)} custom-call(f32[16]{0:T(128)} %occ_ref.1, bf16[16,2,2,128,128]{4,3,2,1,0:T(8,128)(2,1)} %orb_ref.1), custom_call_target="tpu_custom_call" | custom-call | tf_op jit(solution)/shard_map/current/pallas_call | solution.py:235
  36.6 1.5 %copy.4 = f32[3,2,32,128]{3,2,1,0:T(8,128)} copy(f32[3,2,32,128]{3,2,1,0:T(8,128)} %current.1) | data formatting | bytes 196608

commit v2 on v1

--- a/solution.py
+++ b/solution.py
@@ -25,7 +25,7 @@
     nb, ng, occ_ref, orb_ref, out_ref,
     own, mate, outer, mx, my, plane_sum, plane_recv, zsend, zrecv,
     own_sem, mate_send, mate_recv, outer_send, outer_recv,
-    plane_send_sem, plane_recv_sem, z_send_sem, z_recv_sem,
+    plane_send_sem, plane_recv_sem, z_send_sem, z_recv_sem, ready,
 ):
     bands, _, depth, nx, ny = orb_ref.shape
     b = lax.axis_index("band")
@@ -43,15 +43,11 @@
     load.start()
 
     barrier = pltpu.get_barrier_semaphore()
-    count = 0
-    for k in range(nb):
-        peer = lax.rem(b + k, nb)
-        for at in (g, partner, ahead, behind):
-            if k == 0 and at is g:
-                continue
-            pl.semaphore_signal(barrier, inc=1, device_id={"band": peer, "grid": at})
-            count += 1
-    pl.semaphore_wait(barrier, count)
+    peers = [lax.rem(b + k, nb) for k in range(1, nb)]
+    direct = [(b, partner), (b, ahead), (b, behind)] + [(peer, g) for peer in peers]
+    for band, grid in direct:
+        pl.semaphore_signal(barrier, inc=1, device_id={"band": band, "grid": grid})
+    pl.semaphore_wait(barrier, len(direct))
 
     def start_of(chunk, parity):
         block = (chunk // subs) * 2 + parity
@@ -78,6 +74,8 @@
     for c in range(chunks):
         to_mate(c).start()
         to_outer(c).start()
+    for peer in peers:
+        pl.semaphore_signal(ready, inc=1, device_id={"band": peer, "grid": g})
 
     mx[...] = stencil(nx, True)
     my[...] = stencil(ny, False)
@@ -112,6 +110,7 @@
     for k in range(1, nb):
         to_peer(k).start()
 
+    pl.semaphore_wait(ready, nb - 1)
     sign = turn.astype(jnp.float32)
     first = odd
     second = 1 - odd
@@ -259,6 +258,7 @@
                 dma((nb - 1,)),
                 dma((chunks, 3)),
                 dma((2, nb, subs)),
+                pltpu.SemaphoreType.REGULAR,
             ],
             compiler_params=pltpu.CompilerParams(collective_id=0, has_side_effects=True),
             name="current",

time: 38.3 us -> 36.7 us (0.958)
  Pallas kernels: 36.6 us -> 35 us
    pallas_call x1, Pallas kernels: 36.6 us -> 35 us  [per_device(): pl.pallas_call(functools.partial(kernel, nb, ng), out_shape=jax.ShapeDtyp...]
where the time goes in v2:
time: 36.7 us; the launch traced here: 36.6 us
  Pallas kernels  35 us (95%)
  local copies, waits for them, and re-layouts  1.54 us (4%)
    pallas_call x1, Pallas kernels, per_device(): pl.pallas_call(functools.partial(kernel, nb, ng), out_shape=jax.ShapeDtyp...  35 us
    unnamed x1, local copies, waits for them, and re-layouts  1.54 us

profile of v2, /device:TPU:4, one launch (start us, length us, event | category | flops | bytes accessed | tf_op | source)
XLA Modules:
  0.0 36.6 jit_solution(13723633940785078885)
XLA Ops:
  0.0 35.0 %current.1 = f32[3,2,32,128]{3,2,1,0:T(8,128)} custom-call(f32[16]{0:T(128)} %occ_ref.1, bf16[16,2,2,128,128]{4,3,2,1,0:T(8,128)(2,1)} %orb_ref.1), custom_call_target="tpu_custom_call" | custom-call | tf_op jit(solution)/shard_map/current/pallas_call | solution.py:234
  35.0 1.5 %copy.4 = f32[3,2,32,128]{3,2,1,0:T(8,128)} copy(f32[3,2,32,128]{3,2,1,0:T(8,128)} %current.1) | data formatting | bytes 196608

commit v3 on v2

--- a/solution.py
+++ b/solution.py
@@ -127,6 +127,13 @@
         )
 
     for c in range(chunks):
+        if c == chunks - 1:
+            mine = pl.ds(pl.multiple_of(b * rows, rows), rows)
+            summed = plane_sum[:, :, mine, :]
+            for k in range(1, nb):
+                to_peer(k).wait_recv()
+                summed = summed + plane_recv[k - 1]
+            out_ref[1:3] = summed * (1.0 / 12.0)
         start = start_of(c, odd)
         to_mate(c).wait_recv()
         to_outer(c).wait_recv()
@@ -169,13 +176,6 @@
                     here = pl.ds((c % subs) * CHUNK, CHUNK)
                     zrecv[0, b, first, here, :] = parts[0][0]
                     zrecv[0, b, second, here, :] = parts[0][1]
-
-    mine = pl.ds(pl.multiple_of(b * rows, rows), rows)
-    summed = plane_sum[:, :, mine, :]
-    for k in range(1, nb):
-        to_peer(k).wait_recv()
-        summed = summed + plane_recv[k - 1]
-    out_ref[1:3] = summed * (1.0 / 12.0)
 
     def arrival(kind, source):
         for sub in range(subs):
@@ -260,7 +260,7 @@
                 dma((2, nb, subs)),
                 pltpu.SemaphoreType.REGULAR,
             ],
-            compiler_params=pltpu.CompilerParams(collective_id=0, has_side_effects=True),
+            compiler_params=pltpu.CompilerParams(collective_id=0, has_side_effects=True, vmem_limit_bytes=55000 * 1024),
             name="current",
         )(occupations, orbitals)
 

time: 36.7 us -> 35.7 us (0.973)
  Pallas kernels: 35 us -> 34.3 us
    pallas_call x1, Pallas kernels: 35 us -> 34.3 us  [per_device(): pl.pallas_call(functools.partial(kernel, nb, ng), out_shape=jax.ShapeDtyp...]
    unnamed x1 -> x3, local copies, waits for them, and re-layouts: 1.54 us -> 1.3 us
where the time goes in v3:
time: 35.7 us; the launch traced here: 35.6 us
  Pallas kernels  34.3 us (96%)
  local copies, waits for them, and re-layouts  1.3 us (4%)
    pallas_call x1, Pallas kernels, per_device(): pl.pallas_call(functools.partial(kernel, nb, ng), out_shape=jax.ShapeDtyp...  34.3 us
    unnamed x3, local copies, waits for them, and re-layouts  1.3 us

profile of v3, /device:TPU:4, one launch (start us, length us, event | category | flops | bytes accessed | tf_op | source)
XLA Modules:
  0.0 35.6 jit_solution(11764657234781276687)
XLA Ops:
  0.0 0.0 copy-start
  0.0 0.7 %copy-done = f32[16]{0:T(128)S(1)} copy-done((f32[16]{0:T(128)S(1)}, f32[16]{0:T(128)}, u32[]{:S(2)}) %copy-start) | copy-done | bytes 88
  0.7 34.3 %current.1 = f32[3,2,32,128]{3,2,1,0:T(8,128)S(1)} custom-call(f32[16]{0:T(128)S(1)} %copy-done, bf16[16,2,2,128,128]{4,3,2,1,0:T(8,128)(2,1)} %orb_ref.1), custom_call_target="tpu_custom_call" | custom-call | tf_op jit(solution)/shard_map/current/pallas_call | solution.py:234
  34.9 0.6 %copy.4 = f32[3,2,32,128]{3,2,1,0:T(8,128)} copy(f32[3,2,32,128]{3,2,1,0:T(8,128)S(1)} %current.1) | data formatting | bytes 196608
Async XLA Ops:
  0.0 0.7 %copy-start = (f32[16]{0:T(128)S(1)}, f32[16]{0:T(128)}, u32[]{:S(2)}) copy-start(f32[16]{0:T(128)} %occ_ref.1) | copy-start | bytes 196

commit v4 on v3

--- a/solution.py
+++ b/solution.py
@@ -154,7 +154,7 @@
             )
 
         zero = jnp.zeros((CHUNK, ny), jnp.float32)
-        n01, n12, n23, n34, f02, f13, f24, f35 = lax.fori_loop(0, bands, depthwise, (zero,) * 8)
+        n01, n12, n23, n34, f02, f13, f24, f35 = lax.fori_loop(0, bands, depthwise, (zero,) * 8, unroll=4)
         parts = (
             (8.0 * n01 - f02, 8.0 * (n01 + n12) - f13),
             (8.0 * (n12 + n23) - f02 - f24, 8.0 * (n23 + n34) - f13 - f35),

time: 35.7 us -> 35.6 us (level)
  no operation moved by 1% of the time
where the time goes in v4:
time: 35.6 us; the launch traced here: 35.5 us
  Pallas kernels  34.2 us (96%)
  local copies, waits for them, and re-layouts  1.3 us (4%)
    pallas_call x1, Pallas kernels, per_device(): pl.pallas_call(functools.partial(kernel, nb, ng), out_shape=jax.ShapeDtyp...  34.2 us
    unnamed x3, local copies, waits for them, and re-layouts  1.3 us

profile of v4, /device:TPU:4, one launch (start us, length us, event | category | flops | bytes accessed | tf_op | source)
XLA Modules:
  0.0 35.5 jit_solution(3702988830566096770)
XLA Ops:
  0.0 0.0 copy-start
  0.0 0.7 %copy-done = f32[16]{0:T(128)S(1)} copy-done((f32[16]{0:T(128)S(1)}, f32[16]{0:T(128)}, u32[]{:S(2)}) %copy-start) | copy-done | bytes 88
  0.7 34.2 %current.1 = f32[3,2,32,128]{3,2,1,0:T(8,128)S(1)} custom-call(f32[16]{0:T(128)S(1)} %copy-done, bf16[16,2,2,128,128]{4,3,2,1,0:T(8,128)(2,1)} %orb_ref.1), custom_call_target="tpu_custom_call" | custom-call | tf_op jit(solution)/shard_map/current/pallas_call | solution.py:234
  34.8 0.6 %copy.4 = f32[3,2,32,128]{3,2,1,0:T(8,128)} copy(f32[3,2,32,128]{3,2,1,0:T(8,128)S(1)} %current.1) | data formatting | bytes 196608
Async XLA Ops:
  0.0 0.7 %copy-start = (f32[16]{0:T(128)S(1)}, f32[16]{0:T(128)}, u32[]{:S(2)}) copy-start(f32[16]{0:T(128)} %occ_ref.1) | copy-start | bytes 196
